TPU v7x, 32 devices: a whole 2x2x4 slice. The times are simulated.
32 devices in a mesh: member: 2 (over x), dp: 16 (over z, y, core).
Axes of the slice: x: 2, y: 2, z: 4, core: 2. Of those that a mesh axis runs over, the one named last changes fastest.
Arguments:
- residual: bfloat16 [512, 3072], P(('member', 'dp')), parts along dimension 0, may hold values from -6 to 6
- upstream: bfloat16 [512, 3072], P(('member', 'dp')), parts along dimension 0, may hold values from -6 to 6
- gate_weight: bfloat16 [6144, 10240], P('member', 'dp'), parts along dimension 0, may hold values from -0.109375 to 0.109375
- up_weight: bfloat16 [6144, 10240], P('member', 'dp'), parts along dimension 0, may hold values from -0.109375 to 0.109375
- down_weight: bfloat16 [20480, 3072], P(('member', 'dp')), parts along dimension 0, may hold values from -0.0625 to 0.0625
- gain: float32 [6144], P('member'), parts along dimension 0, may hold values from 0.25 to 1.75
Outputs:
- grad_residual: bfloat16 [512, 3072], P(('member', 'dp')), parts along dimension 0
- grad_gate: bfloat16 [6144, 10240], P('member', 'dp'), parts along dimension 0
- grad_up: bfloat16 [6144, 10240], P('member', 'dp'), parts along dimension 0
- grad_down: bfloat16 [20480, 3072], P(('member', 'dp')), parts along dimension 0
- grad_gain: float32 [6144], P('member'), parts along dimension 0
There are 2 independent parts, one for each index of `member`. A program takes and returns all parts, laid end to end along the dimension named above; each array names one. Nothing has to cross between parts.
All inputs are finite; a program needn't handle non-finite values.
Results may differ from a plain program's by a relative error of at most 0.0068.
Values may be sent and summed in bfloat16 or wider, within the bound.
No kernel may reach another device: no remote copies, remote signals or barrier semaphores. Data moves between devices by JAX's collectives and lax.ppermute only.
A program may use at most 128 MiB of HBM per device.

v0:
```python
import jax
import jax.numpy as jnp
from jax import lax
from jax.sharding import PartitionSpec as P

norm_floor = 0.5
gelu_coeff = 0.7978845608
cubic_term = 0.044715


def gelu_parts(gate_out):
    inner = jnp.tanh(gelu_coeff * (gate_out + cubic_term * gate_out * gate_out * gate_out))
    activated = 0.5 * gate_out * (1.0 + inner)
    gelu_slope = 0.5 * (1.0 + inner) + 0.5 * gate_out * (1.0 - inner * inner) * gelu_coeff * (
        1.0 + 3.0 * cubic_term * gate_out * gate_out
    )
    return (activated, gelu_slope)


def contract_last(left, right):
    return lax.dot_general(
        left, right, (((1,), (1,)), ((), ())), preferred_element_type=jnp.float32
    )


def contract_first(left, right):
    return lax.dot_general(
        left, right, (((0,), (0,)), ((), ())), preferred_element_type=jnp.float32
    )


def per_device(residual, upstream, gate_weight, up_weight, down_weight, gain):
    widened = residual.astype(jnp.float32)
    norm_scale = lax.rsqrt(jnp.mean(widened * widened, axis=1, keepdims=True) + norm_floor)
    unit_rows = widened * norm_scale
    normed = (unit_rows * gain).astype(jnp.bfloat16)
    normed_all = lax.all_gather(normed, "dp", axis=0, tiled=True)
    gate_out = jnp.dot(normed_all, gate_weight, preferred_element_type=jnp.float32)
    up_out = jnp.dot(normed_all, up_weight, preferred_element_type=jnp.float32)
    activated, gelu_slope = gelu_parts(gate_out)
    hidden = (activated * up_out).astype(jnp.bfloat16)
    upstream_all = lax.all_gather(upstream, "dp", axis=0, tiled=True)
    hidden_grad = contract_last(upstream_all, down_weight)
    grad_down = contract_first(hidden, upstream_all).astype(jnp.bfloat16)
    gate_grad = (hidden_grad * up_out * gelu_slope).astype(jnp.bfloat16)
    up_grad = (hidden_grad * activated).astype(jnp.bfloat16)
    grad_gate = contract_first(normed_all, gate_grad).astype(jnp.bfloat16)
    grad_up = contract_first(normed_all, up_grad).astype(jnp.bfloat16)
    partial_grad = contract_last(gate_grad, gate_weight) + contract_last(up_grad, up_weight)
    normed_grad = lax.psum_scatter(partial_grad, "dp", scatter_dimension=0, tiled=True)
    unit_grad = normed_grad * gain
    inner_mean = jnp.mean(unit_grad * unit_rows, axis=1, keepdims=True)
    grad_residual = (
        upstream.astype(jnp.float32) + norm_scale * (unit_grad - unit_rows * inner_mean)
    ).astype(jnp.bfloat16)
    grad_gain = lax.psum(jnp.sum(normed_grad * unit_rows, axis=0), "dp")
    return (grad_residual, grad_gate, grad_up, grad_down, grad_gain)


def solution(mesh):
    placed = (
        P(("member", "dp"), None),
        P(("member", "dp"), None),
        P("member", "dp"),
        P("member", "dp"),
        P(("member", "dp"), None),
        P("member"),
    )
    return jax.shard_map(
        per_device,
        mesh=mesh,
        in_specs=placed,
        out_specs=(
            P(("member", "dp"), None),
            P("member", "dp"),
            P("member", "dp"),
            P(("member", "dp"), None),
            P("member"),
        ),
        check_vma=False,
    )
```

profile of v0, /device:TPU:0, one launch (start us, length us, event | category | flops | bytes accessed | tf_op | source)
XLA Modules:
  0.0 235.7 jit_solution(8409215572186535631)
XLA Ops:
  7.2 0.0 all-gather.5.cloned.1.call-start
  7.2 1.0 fusion.18
  8.3 1.6 fusion.11
  9.9 0.0 all-gather.5.cloned.1.call-update
  9.9 0.0 all-gather.3.cloned.1.call-start
  10.0 0.7 all-gather.3.cloned.1.call-update
  10.7 0.0 reduce-scatter.2.cloned.1.call-start
  10.7 42.5 %all-gather.5.cloned.1.call-done = bf16[256,3072]{1,0:T(8,128)(2,1)} async-done(((bf16[16,3072]{1,0:T(8,128)(2,1)}), bf16[256,3072]{1,0:T(8,128)(2,1)}) %all-gather.5.cloned.1.call-update) | async-done | bytes 1572880 | tf_op jit(solution)/shard_map/all_gather | solution.py:37
  53.2 0.0 copy-start
  53.2 0.0 copy-start.2
  53.2 4.1 %fusion.24 = f32[256,640]{1,0:T(8,128)S(1)} fusion(bf16[256,3072]{1,0:T(8,128)(2,1)} %all-gather.5.cloned.1.call-done, bf16[3072,640]{1,0:T(8,128)(2,1)} %param.8), kind=kOutput, calls=%fused_computation.37 | convolution fusion | flops 1006632960 | bytes 6160384 | tf_op jit(solution)/shard_map/dot_general | solution.py:38
  57.3 0.0 copy-done
  57.3 0.1 copy-done.2
  57.4 1.5 fusion.23
  58.9 34.9 %all-gather.3.cloned.1.call-done = bf16[256,3072]{1,0:T(8,128)(2,1)} async-done(((bf16[16,3072]{1,0:T(8,128)(2,1)}), bf16[256,3072]{1,0:T(8,128)(2,1)}) %all-gather.3.cloned.1.call-update) | async-done | bytes 1572880 | tf_op jit(solution)/shard_map/all_gather | solution.py:42
  93.8 0.0 copy-start.1
  93.8 4.4 %multiply_convert_fusion.1 = (bf16[256,640]{1,0:T(8,128)(2,1)S(1)}, bf16[256,640]{1,0:T(8,128)(2,1)S(1)}) fusion(f32[256,640]{1,0:T(8,128)S(1)} %fusion.24, f32[256,640]{1,0:T(8,128)S(1)} %fusion.23, bf16[256,3072]{1,0:T(8,128)(2,1)} %all-gather.3.cloned.1.call-done, bf16[640,3072]{1,0:T(8,128)(2,1)} %param.10), kind=kOutput, calls=%fused_computation.14 | convolution fusion | flops 1010401280 | bytes 7471104 | tf_op jit(solution)/shard_map/dot_general | solution.py:21
  98.3 0.0 copy-start.3
  98.3 0.0 copy-done.1
  98.3 1.4 fusion.25
  99.7 0.7 copy-done.3
  100.4 3.1 %convolution_add_fusion = f32[256,3072]{1,0:T(8,128)} fusion(f32[256,3072]{1,0:T(8,128)S(1)} %fusion.25, bf16[256,640]{1,0:T(8,128)(2,1)S(1)} %get-tuple-element.7, bf16[3072,640]{1,0:T(8,128)(2,1)S(1)} %copy-done.3), kind=kOutput, calls=%fused_computation.3 | convolution fusion | flops 1007419392 | bytes 10551296 | tf_op jit(solution)/shard_map/dot_general | solution.py:21
  103.4 0.0 reduce-scatter.2.cloned.1.call-update
  103.5 3.4 %convolution_convert_fusion.1 = bf16[3072,640]{1,0:T(8,128)(2,1)} fusion(bf16[256,3072]{1,0:T(8,128)(2,1)S(1)} %copy-done, bf16[256,640]{1,0:T(8,128)(2,1)S(1)} %get-tuple-element.7), kind=kOutput, calls=%fused_computation.1 | convolution fusion | flops 1008599040 | bytes 5832704 | tf_op jit(solution)/shard_map/dot_general | solution.py:27
  106.8 0.0 copy-start.5
  106.8 3.4 %convolution_convert_fusion.2 = bf16[3072,640]{1,0:T(8,128)(2,1)} fusion(bf16[256,3072]{1,0:T(8,128)(2,1)S(1)} %copy-done, bf16[256,640]{1,0:T(8,128)(2,1)S(1)} %get-tuple-element.8), kind=kOutput, calls=%fused_computation.2 | convolution fusion | flops 1008599040 | bytes 5832704 | tf_op jit(solution)/shard_map/dot_general | solution.py:27
  110.2 0.0 copy-done.5
  110.2 0.0 copy-start.4
  110.2 0.0 copy-start.7
  110.2 0.0 copy-start.6
  110.2 3.3 %convolution_convert_fusion = bf16[640,3072]{1,0:T(8,128)(2,1)} fusion(bf16[256,3072]{1,0:T(8,128)(2,1)S(1)} %copy-done.5, f32[256,640]{1,0:T(8,128)S(1)} %fusion.23, f32[256,640]{1,0:T(8,128)S(1)} %fusion.24), kind=kOutput, calls=%fused_computation | convolution fusion | flops 1010237440 | bytes 6815744 | tf_op jit(solution)/shard_map/dot_general | solution.py:27
  113.5 55.1 %reduce-scatter.2.cloned.1.call-done = f32[16,3072]{1,0:T(8,128)} async-done(((f32[256,3072]{1,0:T(8,128)}), f32[16,3072]{1,0:T(8,128)}) %reduce-scatter.2.cloned.1.call-update) | async-done | bytes 196624 | tf_op jit(solution)/shard_map/reduce_scatter | solution.py:50
  168.6 0.0 copy-done.4
  168.6 0.0 copy-done.7
  168.6 1.2 fusion.17
  169.8 57.7 %psum.7 = f32[3072]{0:T(1024)} all-reduce(f32[3072]{0:T(1024)S(1)} %get-tuple-element.5), channel_id=1, replica_groups=mesh['member'=2,'dp'=16] {'dp'}, use_global_device_ids=true, to_apply=%region_4.0 | all-reduce | flops 3072 | bytes 24576 | tf_op jit(solution)/shard_map/psum | solution.py:56
  227.5 0.0 copy-done.6
  227.5 1.7 fusion.16
  (2 shorter events, 0.0 us)
Async XLA Ops:
  7.2 46.0 %all-gather.5.cloned.1.call-start = ((), (), s32[]{:S(2)}) async-start(), calls=%async_computation.2 | async-start | bytes 1671168 | tf_op jit(solution)/shard_map/all_gather | solution.py:37
  9.9 83.9 %all-gather.3.cloned.1.call-start = ((), (), s32[]{:S(2)}) async-start(), calls=%async_computation.1 | async-start | bytes 1671168 | tf_op jit(solution)/shard_map/all_gather | solution.py:42
  10.7 158.0 %reduce-scatter.2.cloned.1.call-start = ((), (), s32[]{:S(2)}) async-start(), calls=%async_computation.3 | async-start | bytes 3342336 | tf_op jit(solution)/shard_map/reduce_scatter | solution.py:50
  53.2 4.1 %copy-start = (bf16[256,3072]{1,0:T(8,128)(2,1)S(1)}, bf16[256,3072]{1,0:T(8,128)(2,1)}, u32[]{:S(2)}) copy-start(bf16[256,3072]{1,0:T(8,128)(2,1)} %all-gather.5.cloned.1.call-done) | copy-start | bytes 4718596
  53.2 4.2 %copy-start.2 = (bf16[3072,640]{1,0:T(8,128)(2,1)S(1)}, bf16[3072,640]{1,0:T(8,128)(2,1)}, u32[]{:S(2)}) copy-start(bf16[3072,640]{1,0:T(8,128)(2,1)} %param.9) | copy-start | bytes 11796484
  93.8 4.5 %copy-start.1 = (bf16[3072,640]{1,0:T(8,128)(2,1)S(1)}, bf16[3072,640]{1,0:T(8,128)(2,1)}, u32[]{:S(2)}) copy-start(bf16[3072,640]{1,0:T(8,128)(2,1)} %param.8) | copy-start | bytes 11796484
  98.3 2.1 copy-start.3
  106.8 3.4 %copy-start.5 = (bf16[256,3072]{1,0:T(8,128)(2,1)S(1)}, bf16[256,3072]{1,0:T(8,128)(2,1)}, u32[]{:S(2)}) copy-start(bf16[256,3072]{1,0:T(8,128)(2,1)} %all-gather.3.cloned.1.call-done) | copy-start | bytes 4718596
  110.2 58.4 %copy-start.4 = (bf16[16,3072]{1,0:T(8,128)(2,1)S(1)}, bf16[16,3072]{1,0:T(8,128)(2,1)}, u32[]{:S(2)}) copy-start(bf16[16,3072]{1,0:T(8,128)(2,1)} %param.6) | copy-start | bytes 294916
  110.2 58.4 %copy-start.7 = (f32[3072]{0:T(1024)S(1)}, f32[3072]{0:T(1024)}, u32[]{:S(2)}) copy-start(f32[3072]{0:T(1024)} %param.11) | copy-start | bytes 36868
  110.2 117.3 %copy-start.6 = (bf16[16,3072]{1,0:T(8,128)(2,1)S(1)}, bf16[16,3072]{1,0:T(8,128)(2,1)}, u32[]{:S(2)}) copy-start(bf16[16,3072]{1,0:T(8,128)(2,1)} %param.7) | copy-start | bytes 294916
Sparse Core Ops, SparseCore 0:
  10.8 42.3 all-gather.4
  55.5 38.2 all-gather.2
  103.6 64.9 reduce-scatter.1
where the time goes:
time: 236 us
  waiting for transfers between devices  133 us (56%)
  blocking collectives  57.7 us (24%)
  matrix products  24.5 us (10%)
  between operations  13.8 us (6%)
  other arithmetic  5.52 us (2%)
    psum x1, blocking collectives, per_device(): grad_gain = lax.psum(jnp.sum(normed_grad * unit_rows, axis=0), 'dp')  57.7 us
    reduce_scatter x1, waiting for transfers between devices, per_device(): lax.psum_scatter(partial_grad, 'dp', scatter_dimension=0, tiled=True)  55.1 us
    all_gather x1, waiting for transfers between devices, per_device(): normed_all = lax.all_gather(normed, 'dp', axis=0, tiled=True)  42.5 us
    all_gather x1, waiting for transfers between devices, per_device(): upstream_all = lax.all_gather(upstream, 'dp', axis=0, tiled=True)  34.9 us
    dot_general x3, matrix products, contract_first(): lax.dot_general(left, right, (((0,), (0,)), ((), ())), preferred_element_...  10.1 us
    dot_general x3, matrix products, contract_last(): lax.dot_general(left, right, (((1,), (1,)), ((), ())), preferred_element_...  8.91 us
  transfers between devices with their start and end apart: 3, of which 3 were waited for; matrix products, arithmetic and copies ran while one was open for 7% of the time, Pallas kernels for 0%

commit v1 on v0

--- a/solution.py
+++ b/solution.py
@@ -53,7 +53,7 @@
     grad_residual = (
         upstream.astype(jnp.float32) + norm_scale * (unit_grad - unit_rows * inner_mean)
     ).astype(jnp.bfloat16)
-    grad_gain = lax.psum(jnp.sum(normed_grad * unit_rows, axis=0), "dp")
+    grad_gain = jnp.sum(lax.all_gather(jnp.sum(normed_grad * unit_rows, axis=0), "dp"), axis=0)
     return (grad_residual, grad_gate, grad_up, grad_down, grad_gain)
 
 

time: 236 us -> 199 us (0.84)
  blocking collectives: 57.7 us -> 19.9 us
    psum x1 -> x0, blocking collectives: 57.7 us -> none  [per_device(): grad_gain = lax.psum(jnp.sum(normed_grad * unit_rows, axis=0), 'dp')]
    all_gather x0 -> x1, blocking collectives: none -> 19.9 us  [per_device(): lax.all_gather(jnp.sum(normed_grad * unit_rows, axis=0), 'dp')]
  transfers between devices with their start and end apart: 3 -> 3, of which waited for: 3 -> 3; matrix products, arithmetic and copies ran while one was open for 7% -> 8% of each run, Pallas kernels for 0% -> 0%
where the time goes in v1:
time: 199 us
  waiting for transfers between devices  133 us (67%)
  matrix products  24.5 us (12%)
  blocking collectives  19.9 us (10%)
  between operations  13.8 us (7%)
  other arithmetic  6.16 us (3%)
    reduce_scatter x1, waiting for transfers between devices, per_device(): lax.psum_scatter(partial_grad, 'dp', scatter_dimension=0, tiled=True)  55.1 us
    all_gather x1, waiting for transfers between devices, per_device(): normed_all = lax.all_gather(normed, 'dp', axis=0, tiled=True)  42.5 us
    all_gather x1, waiting for transfers between devices, per_device(): upstream_all = lax.all_gather(upstream, 'dp', axis=0, tiled=True)  34.9 us
    all_gather x1, blocking collectives, per_device(): lax.all_gather(jnp.sum(normed_grad * unit_rows, axis=0), 'dp')  19.9 us
    dot_general x3, matrix products, contract_first(): lax.dot_general(left, right, (((0,), (0,)), ((), ())), preferred_element_...  10.1 us
    dot_general x3, matrix products, contract_last(): lax.dot_general(left, right, (((1,), (1,)), ((), ())), preferred_element_...  8.91 us
    dot_general x1, matrix products, per_device(): jnp.dot(normed_all, gate_weight, preferred_element_type=jnp.float32)  4.12 us
  transfers between devices with their start and end apart: 3, of which 3 were waited for; matrix products, arithmetic and copies ran while one was open for 8% of the time, Pallas kernels for 0%

profile of v1, /device:TPU:0, one launch (start us, length us, event | category | flops | bytes accessed | tf_op | source)
XLA Modules:
  0.0 198.6 jit_solution(14411506833017218460)
XLA Ops:
  7.2 0.0 all-gather.6.cloned.1.call-start
  7.2 1.0 fusion.18
  8.3 1.6 fusion.11
  9.9 0.0 all-gather.6.cloned.1.call-update
  9.9 0.0 all-gather.4.cloned.1.call-start
  10.0 0.7 all-gather.4.cloned.1.call-update
  10.7 0.0 reduce-scatter.2.cloned.1.call-start
  10.7 42.5 %all-gather.6.cloned.1.call-done = bf16[256,3072]{1,0:T(8,128)(2,1)} async-done(((bf16[16,3072]{1,0:T(8,128)(2,1)}), bf16[256,3072]{1,0:T(8,128)(2,1)}) %all-gather.6.cloned.1.call-update) | async-done | bytes 1572880 | tf_op jit(solution)/shard_map/all_gather | solution.py:37
  53.2 0.0 copy-start
  53.2 0.0 copy-start.2
  53.2 4.1 %fusion.24 = f32[256,640]{1,0:T(8,128)S(1)} fusion(bf16[256,3072]{1,0:T(8,128)(2,1)} %all-gather.6.cloned.1.call-done, bf16[3072,640]{1,0:T(8,128)(2,1)} %param.8), kind=kOutput, calls=%fused_computation.37 | convolution fusion | flops 1006632960 | bytes 6160384 | tf_op jit(solution)/shard_map/dot_general | solution.py:38
  57.3 0.0 copy-done
  57.3 0.1 copy-done.2
  57.4 1.5 fusion.23
  58.9 34.9 %all-gather.4.cloned.1.call-done = bf16[256,3072]{1,0:T(8,128)(2,1)} async-done(((bf16[16,3072]{1,0:T(8,128)(2,1)}), bf16[256,3072]{1,0:T(8,128)(2,1)}) %all-gather.4.cloned.1.call-update) | async-done | bytes 1572880 | tf_op jit(solution)/shard_map/all_gather | solution.py:42
  93.8 0.0 copy-start.1
  93.8 4.4 %multiply_convert_fusion.1 = (bf16[256,640]{1,0:T(8,128)(2,1)S(1)}, bf16[256,640]{1,0:T(8,128)(2,1)S(1)}) fusion(f32[256,640]{1,0:T(8,128)S(1)} %fusion.24, f32[256,640]{1,0:T(8,128)S(1)} %fusion.23, bf16[256,3072]{1,0:T(8,128)(2,1)} %all-gather.4.cloned.1.call-done, bf16[640,3072]{1,0:T(8,128)(2,1)} %param.10), kind=kOutput, calls=%fused_computation.14 | convolution fusion | flops 1010401280 | bytes 7471104 | tf_op jit(solution)/shard_map/dot_general | solution.py:21
  98.3 0.0 copy-start.3
  98.3 0.0 copy-done.1
  98.3 1.4 fusion.25
  99.7 0.7 copy-done.3
  100.4 3.1 %convolution_add_fusion = f32[256,3072]{1,0:T(8,128)} fusion(f32[256,3072]{1,0:T(8,128)S(1)} %fusion.25, bf16[256,640]{1,0:T(8,128)(2,1)S(1)} %get-tuple-element.7, bf16[3072,640]{1,0:T(8,128)(2,1)S(1)} %copy-done.3), kind=kOutput, calls=%fused_computation.3 | convolution fusion | flops 1007419392 | bytes 10551296 | tf_op jit(solution)/shard_map/dot_general | solution.py:21
  103.4 0.0 reduce-scatter.2.cloned.1.call-update
  103.5 3.4 %convolution_convert_fusion.1 = bf16[3072,640]{1,0:T(8,128)(2,1)} fusion(bf16[256,3072]{1,0:T(8,128)(2,1)S(1)} %copy-done, bf16[256,640]{1,0:T(8,128)(2,1)S(1)} %get-tuple-element.7), kind=kOutput, calls=%fused_computation.1 | convolution fusion | flops 1008599040 | bytes 5832704 | tf_op jit(solution)/shard_map/dot_general | solution.py:27
  106.8 0.0 copy-start.5
  106.8 3.4 %convolution_convert_fusion.2 = bf16[3072,640]{1,0:T(8,128)(2,1)} fusion(bf16[256,3072]{1,0:T(8,128)(2,1)S(1)} %copy-done, bf16[256,640]{1,0:T(8,128)(2,1)S(1)} %get-tuple-element.8), kind=kOutput, calls=%fused_computation.2 | convolution fusion | flops 1008599040 | bytes 5832704 | tf_op jit(solution)/shard_map/dot_general | solution.py:27
  110.2 0.0 copy-done.5
  110.2 0.0 copy-start.4
  110.2 0.0 copy-start.7
  110.2 0.0 copy-start.6
  110.2 3.3 %convolution_convert_fusion = bf16[640,3072]{1,0:T(8,128)(2,1)} fusion(bf16[256,3072]{1,0:T(8,128)(2,1)S(1)} %copy-done.5, f32[256,640]{1,0:T(8,128)S(1)} %fusion.23, f32[256,640]{1,0:T(8,128)S(1)} %fusion.24), kind=kOutput, calls=%fused_computation | convolution fusion | flops 1010237440 | bytes 6815744 | tf_op jit(solution)/shard_map/dot_general | solution.py:27
  113.5 55.1 %reduce-scatter.2.cloned.1.call-done = f32[16,3072]{1,0:T(8,128)} async-done(((f32[256,3072]{1,0:T(8,128)}), f32[16,3072]{1,0:T(8,128)}) %reduce-scatter.2.cloned.1.call-update) | async-done | bytes 196624 | tf_op jit(solution)/shard_map/reduce_scatter | solution.py:50
  168.6 0.0 copy-done.4
  168.6 0.0 copy-done.7
  168.6 1.2 fusion.17
  169.8 19.9 %all-gather = f32[49152]{0:T(1024)S(1)} all-gather(f32[3072]{0:T(1024)S(1)} %get-tuple-element.5), channel_id=2, replica_groups=mesh['member'=2,'dp'=16] {'dp'}, dimensions={0}, use_global_device_ids=true | all-gather | bytes 208896 | tf_op jit(solution)/shard_map/all_gather | solution.py:56
  189.7 0.6 reduce_sum.39
  190.3 0.0 copy-done.6
  190.3 1.7 fusion.16
  (3 shorter events, 0.1 us)
Async XLA Ops:
  7.2 46.0 %all-gather.6.cloned.1.call-start = ((), (), s32[]{:S(2)}) async-start(), calls=%async_computation.2 | async-start | bytes 1671168 | tf_op jit(solution)/shard_map/all_gather | solution.py:37
  9.9 83.9 %all-gather.4.cloned.1.call-start = ((), (), s32[]{:S(2)}) async-start(), calls=%async_computation.1 | async-start | bytes 1671168 | tf_op jit(solution)/shard_map/all_gather | solution.py:42
  10.7 158.0 %reduce-scatter.2.cloned.1.call-start = ((), (), s32[]{:S(2)}) async-start(), calls=%async_computation.3 | async-start | bytes 3342336 | tf_op jit(solution)/shard_map/reduce_scatter | solution.py:50
  53.2 4.1 %copy-start = (bf16[256,3072]{1,0:T(8,128)(2,1)S(1)}, bf16[256,3072]{1,0:T(8,128)(2,1)}, u32[]{:S(2)}) copy-start(bf16[256,3072]{1,0:T(8,128)(2,1)} %all-gather.6.cloned.1.call-done) | copy-start | bytes 4718596
  53.2 4.2 %copy-start.2 = (bf16[3072,640]{1,0:T(8,128)(2,1)S(1)}, bf16[3072,640]{1,0:T(8,128)(2,1)}, u32[]{:S(2)}) copy-start(bf16[3072,640]{1,0:T(8,128)(2,1)} %param.9) | copy-start | bytes 11796484
  93.8 4.5 %copy-start.1 = (bf16[3072,640]{1,0:T(8,128)(2,1)S(1)}, bf16[3072,640]{1,0:T(8,128)(2,1)}, u32[]{:S(2)}) copy-start(bf16[3072,640]{1,0:T(8,128)(2,1)} %param.8) | copy-start | bytes 11796484
  98.3 2.1 %copy-start.3 = (bf16[3072,640]{1,0:T(8,128)(2,1)S(1)}, bf16[3072,640]{1,0:T(8,128)(2,1)}, u32[]{:S(2)}) copy-start(bf16[3072,640]{1,0:T(8,128)(2,1)} %param.9) | copy-start | bytes 11796484
  106.8 3.4 %copy-start.5 = (bf16[256,3072]{1,0:T(8,128)(2,1)S(1)}, bf16[256,3072]{1,0:T(8,128)(2,1)}, u32[]{:S(2)}) copy-start(bf16[256,3072]{1,0:T(8,128)(2,1)} %all-gather.4.cloned.1.call-done) | copy-start | bytes 4718596
  110.2 58.4 %copy-start.4 = (bf16[16,3072]{1,0:T(8,128)(2,1)S(1)}, bf16[16,3072]{1,0:T(8,128)(2,1)}, u32[]{:S(2)}) copy-start(bf16[16,3072]{1,0:T(8,128)(2,1)} %param.6) | copy-start | bytes 294916
  110.2 58.4 %copy-start.7 = (f32[3072]{0:T(1024)S(1)}, f32[3072]{0:T(1024)}, u32[]{:S(2)}) copy-start(f32[3072]{0:T(1024)} %param.11) | copy-start | bytes 36868
  110.2 80.1 %copy-start.6 = (bf16[16,3072]{1,0:T(8,128)(2,1)S(1)}, bf16[16,3072]{1,0:T(8,128)(2,1)}, u32[]{:S(2)}) copy-start(bf16[16,3072]{1,0:T(8,128)(2,1)} %param.7) | copy-start | bytes 294916
Sparse Core Ops, SparseCore 0:
  10.8 42.3 all-gather.5
  55.5 38.2 all-gather.3
  103.6 64.9 reduce-scatter.1
